TPU v7x, 32 devices: a whole 2x2x4 slice. The times are simulated.
32 devices in a mesh: grp: 8 (over z, y), rep: 4 (over x, core).
Axes of the slice: x: 2, y: 2, z: 4, core: 2. Of those that a mesh axis runs over, the one named last changes fastest.
Arguments:
- queries: bfloat16 [16, 4, 32, 128], P('grp', 'rep'), may hold values from -3.2 to 3.2
- passages: bfloat16 [512, 4, 180, 128], P('grp', 'rep'), may hold values from -1.796875 to 1.796875
- lengths: int32 [512, 4], P('grp', 'rep'), may hold values from 16 to 180
- cand_ids: int32 [16, 4, 64], P('grp', 'rep'), may hold values from 0 to 511, as said below
- owner_map: int32 [4, 512], P('rep'), may hold values from 0 to 511, as said below
- teacher: float32 [16, 4, 64], P('grp', 'rep'), may hold values from -12 to 312
- weights: float32 [16, 4], P('grp', 'rep'), may hold values from 0.5 to 18
Outputs:
- loss: float32 [], replicated
- query_grad: float32 [16, 4, 32, 128], P('grp', 'rep')
- passage_grad: bfloat16 [512, 4, 180, 128], P('grp', 'rep')
Inputs may be any that keep to these rules, and one draw needn't show every extreme that they name: `cand_ids`: within each replica, the 128 candidates of the queries of one grp index have storage rows of which at most 32 (counted with repeats) lie in any one aligned block of 64 rows; in every draw, in each replica, one block receives exactly 32 from every grp index. `owner_map`: each row is a permutation of 0 to 511.
All inputs are finite; a program needn't handle non-finite values.
Results may differ from a plain program's by a relative error of at most 0.0055.
Values may be sent and summed in bfloat16 or wider, within the bound.
No kernel may reach another device: no remote copies, remote signals or barrier semaphores. Data moves between devices by JAX's collectives and lax.ppermute only.
A program may use at most 128 MiB of HBM per device.

v0:
```python
import functools
import math

import jax
import jax.numpy as jnp
from jax import lax
from jax.experimental import pallas as pl
from jax.experimental.pallas import tpu as pltpu
from jax.sharding import PartitionSpec as P


TEMPER = 0.05
LOG2E = math.log2(math.e)
MASKED = -1e30
KINDS = 8
UNROLL = 14
SPREAD = 5
SUMS = 4
STORE = 5
PIECES = 4
HIGHEST = lax.Precision.HIGHEST
VMEM = pltpu.VMEM
SMEM = pltpu.SMEM


def round_up(value, multiple):
    return -(-value // multiple) * multiple


def iota(shape, dim):
    return lax.broadcasted_iota(jnp.int32, shape, dim)


def three_parts(values):
    first = values.astype(jnp.bfloat16).astype(jnp.float32)
    rest = values - first
    second = rest.astype(jnp.bfloat16).astype(jnp.float32)
    third = (rest - second).astype(jnp.bfloat16).astype(jnp.float32)
    return first, second, third


def pack_kernel(passage_local, queries, cand_ids, owner_map, teacher, weights, out, aux):
    groups = out.shape[0]
    tokens = queries.shape[0]
    query_local, _, candidates = cand_ids.shape
    entries = owner_map.shape[1]
    table = owner_map[...].astype(jnp.float32)
    owner = jnp.floor((table + 0.5) * (1.0 / passage_local))
    local = table - owner * passage_local
    which = iota((8, entries), 0)
    tables = jnp.where(which == 0, owner, jnp.where(which == 1, local, 0.0)).astype(jnp.bfloat16)
    aux[...] = jnp.zeros_like(aux)
    for q in range(query_local):
        hot = (iota((entries, candidates), 0) == cand_ids[q]).astype(jnp.bfloat16)
        found = jnp.dot(tables, hot, preferred_element_type=jnp.float32)
        scores = teacher[q]
        shifted = scores - jnp.max(scores, axis=1, keepdims=True)
        log_teacher = shifted - jnp.log(jnp.sum(jnp.exp(shifted), axis=1, keepdims=True))
        weight = jnp.broadcast_to(weights[:, q : q + 1], (1, candidates))
        rows = (found[0:1], found[1:2], *three_parts(log_teacher), *three_parts(weight))
        for kind, row in enumerate(rows):
            at = kind * query_local + q
            aux[at : at + 1, 0:candidates] = row
    packed = aux[...].astype(jnp.bfloat16)
    for g in range(groups):
        out[g, 0:tokens, :] = queries[...]
        out[g, tokens:, :] = packed


def owned_rows(arrived, tokens, query_local, candidates, g, q, me):
    at = tokens + q
    owner = arrived[g, at : at + 1, 0:candidates].astype(jnp.float32)
    at = tokens + query_local + q
    local = arrived[g, at : at + 1, 0:candidates].astype(jnp.float32)
    return jnp.where(owner == me.astype(jnp.float32), local, -1.0).astype(jnp.int32)


def prepare_kernel(stored_hbm, rows_hbm, stored, gathered, rows, stored_done, rows_done):
    token_len, chunk, feature = stored.shape
    padded = rows.shape[1]
    pitch = gathered.shape[0] // chunk
    pieces = stored_done.shape[0]
    piece = token_len // pieces
    spans = [(k * piece, token_len if k == pieces - 1 else (k + 1) * piece) for k in range(pieces)]
    copies = []
    for k, (first, last) in enumerate(spans):
        at = pl.ds(first, last - first)
        copies.append(pltpu.make_async_copy(stored_hbm.at[at], stored.at[at], stored_done.at[k]))
        copies[-1].start()

    def clear(p, carry):
        at = pl.ds(p * pitch + token_len, padded - token_len)
        gathered[at, :] = jnp.zeros((padded - token_len, feature), jnp.float32)
        return carry

    lax.fori_loop(0, chunk, clear, 0)
    for copy, (first, last) in zip(copies, spans):
        copy.wait()

        def spread(j, carry, first=first):
            for u in range(SPREAD):
                at = first + j * SPREAD + u
                gathered[pl.ds(at, chunk, stride=pitch), :] = stored[at].astype(jnp.float32)
            return carry

        whole = (last - first) // SPREAD
        lax.fori_loop(0, whole, spread, 0)
        for at in range(first + whole * SPREAD, last):
            gathered[pl.ds(at, chunk, stride=pitch), :] = stored[at].astype(jnp.float32)

    parts = rows_done.shape[0]
    part = chunk // parts
    ahead = math.gcd(part, 4)
    copies = []
    for k in range(parts):

        def collect(step, carry, first=k * part):
            for inner in range(ahead):
                p = first + step * ahead + inner
                rows[p] = gathered[pl.ds(p * pitch, padded), :].astype(jnp.bfloat16)
            return carry

        lax.fori_loop(0, part // ahead, collect, 0)
        at = pl.ds(k * part, part)
        copies.append(pltpu.make_async_copy(rows.at[at], rows_hbm.at[at], rows_done.at[k]))
        copies[-1].start()
    for copy in copies:
        copy.wait()


def list_blocks(flags_scalar, block_code, block_count, passage_count, tiles):
    base = code_base(tiles)
    ahead = math.gcd(passage_count, 4)

    def list_passages(step, count):
        for inner in range(ahead):
            p = step * ahead + inner
            for tile in range(tiles):
                block_code[0, count] = p * base + tile
                count = count + flags_scalar[p, tile]
        return count

    count = lax.fori_loop(0, passage_count // ahead, list_passages, jnp.int32(0))
    for extra in range(3 * UNROLL):
        block_code[0, count + extra] = passage_count * base
    steps = (count + 2 * UNROLL - 1) // (2 * UNROLL)
    block_count[0, 0] = steps
    return steps


def code_base(tiles):
    return 1 << (tiles - 1).bit_length()


def decode(block_code, block, tiles):
    code = block_code[0, block]
    base = code_base(tiles)
    return code >> (base.bit_length() - 1), code & (base - 1)


def score_kernel(
    dims,
    axis,
    arrived,
    lengths,
    *refs,
):
    tokens, query_local, candidates, per_tile, replicas = dims
    weights, refs = refs[:replicas], refs[replicas:]
    passages_hbm, scores_out, summed, block_code, block_count, powers_hbm, *scratch = refs
    score_body(
        (tokens, query_local, candidates, per_tile),
        lax.axis_index(axis),
        arrived,
        lengths,
        pair_sums([one[...] for one in weights]),
        passages_hbm,
        scores_out,
        summed,
        block_code,
        block_count,
        powers_hbm,
        *scratch,
    )


def score_body(
    dims,
    me,
    arrived,
    lengths,
    weights,
    passages_hbm,
    scores_out,
    summed,
    block_code,
    block_count,
    powers_hbm,
    highest,
    passages,
    turned,
    flags,
    flags_scalar,
    penalty,
    even,
    odd,
    even_top,
    odd_top,
    powers,
    flags_done,
    rows_done,
    powers_done,
):
    tokens, query_local, candidates, per_tile = dims
    groups = arrived.shape[0]
    passage_count, padded, _ = passages.shape
    tiles, _, lanes = highest.shape
    groups_per_tile = per_tile // query_local
    fetch_rows = pltpu.make_async_copy(passages_hbm, passages, rows_done)
    fetch_rows.start()

    column = iota(flags.shape, 1)
    passage_index = iota((passage_count, candidates), 0)
    marks = jnp.zeros(flags.shape, jnp.int32)
    for tile in range(tiles):
        hit = jnp.zeros((passage_count, candidates), jnp.int32)
        for g in range(tile * groups_per_tile, (tile + 1) * groups_per_tile):
            for q in range(query_local):
                mine = owned_rows(arrived, tokens, query_local, candidates, g, q, me)
                hit = jnp.where(passage_index == mine, 1, hit)
        any_hit = jnp.max(hit, axis=1, keepdims=True)
        marks = jnp.where(column == tile, any_hit, marks)
    flags[...] = marks
    to_scalar = pltpu.make_async_copy(flags, flags_scalar, flags_done)
    to_scalar.start()

    for tile in range(tiles):
        parts = [
            arrived[g, 0:tokens, :]
            for g in range(tile * groups_per_tile, (tile + 1) * groups_per_tile)
        ]
        block = jnp.concatenate(parts, axis=0).astype(jnp.float32)
        turned[tile] = block.T.astype(jnp.bfloat16)
    highest[...] = jnp.zeros_like(highest)
    summed[...] = jnp.ones_like(summed)
    penalty[...] = jnp.where(iota(penalty.shape, 0) < padded, 0.0, MASKED)
    to_scalar.wait()
    steps = list_blocks(flags_scalar, block_code, block_count, passage_count, tiles)
    fetch_rows.wait()

    factor = LOG2E / TEMPER

    def multiply(first, into, tops):
        for u in range(UNROLL):
            slot, tile = decode(block_code, first + u, tiles)
            p = jnp.minimum(slot, passage_count - 1)
            products = jnp.dot(passages[p], turned[tile], preferred_element_type=jnp.float32)
            products = products + penalty[pl.ds(padded - lengths[0, p], padded), :]
            into[u] = products
            tops[u : u + 1, :] = jnp.max(products, axis=0, keepdims=True)

    def soften(first, held, tops):
        for u in range(UNROLL):
            slot, tile = decode(block_code, first + u, tiles)
            top = tops[u : u + 1, :]
            raised = jnp.exp2((held[u] - top) * factor)
            powers[first + u] = raised.astype(jnp.bfloat16)
            highest[tile, pl.ds(slot, 1), :] = top
            summed[tile, pl.ds(slot, 1), :] = jnp.sum(raised, axis=0, keepdims=True)

    def chunk_copy(s):
        at = pl.ds(s * 2 * UNROLL, 2 * UNROLL)
        return pltpu.make_async_copy(powers.at[at], powers_hbm.at[at], powers_done.at[s])

    multiply(0, even, even_top)

    def step(s, carry):
        first = s * 2 * UNROLL
        multiply(first + UNROLL, odd, odd_top)
        soften(first, even, even_top)
        multiply(first + 2 * UNROLL, even, even_top)
        soften(first + UNROLL, odd, odd_top)
        chunk_copy(s).start()
        return carry

    lax.fori_loop(0, steps, step, 0)

    query_len = lanes // per_tile
    member = iota((lanes, 128), 0) // query_len == iota((lanes, 128), 1)
    member = member.astype(jnp.float32)
    weight_part = jnp.sum(weights, axis=1, keepdims=True)
    scores_out[0] = jnp.broadcast_to(weight_part, scores_out.shape[1:])
    for tile in range(tiles):
        matched = highest[tile, 0:passage_count, :] + TEMPER * jnp.log(
            summed[tile, 0:passage_count, :]
        )
        sums = jnp.dot(matched, member, precision=HIGHEST, preferred_element_type=jnp.float32)
        for inner in range(per_tile):
            g = tile * groups_per_tile + inner // query_local
            q = inner % query_local
            mine = owned_rows(arrived, tokens, query_local, candidates, g, q, me)
            picked = jnp.where(passage_index == mine, sums[:, inner : inner + 1], 0.0)
            at = tile * per_tile + inner
            scores_out[0, at : at + 1, 0:candidates] = jnp.sum(picked, axis=0, keepdims=True)
    for g in range(1, groups):
        scores_out[g] = scores_out[0]

    def finish(s, carry):
        chunk_copy(s).wait()
        return carry

    lax.fori_loop(0, steps, finish, 0)


def pair_sums(values):
    while len(values) > 1:
        values = [values[i] + values[i + 1] for i in range(0, len(values), 2)]
    return values[0]


def query_kernel(
    dims,
    axis,
    arrived,
    scores,
    summed,
    block_code,
    block_count,
    passages_hbm,
    powers_hbm,
    grads_out,
    multiplier,
    numerator_out,
    weight_sum_out,
    passages,
    powers,
    factors,
    rows_done,
    powers_done,
    *sums,
):
    tokens, query_local, candidates, per_tile, query_total = dims
    groups = arrived.shape[0]
    tiles, slots, lanes = summed.shape
    passage_count = passages.shape[0]
    groups_per_tile = per_tile // query_local
    queries_all = tiles * per_tile
    query_len = lanes // per_tile
    me = lax.axis_index(axis)
    steps = block_count[0, 0]
    fetch_rows = pltpu.make_async_copy(passages_hbm, passages, rows_done)
    fetch_rows.start()

    def chunk_copy(s):
        at = pl.ds(s * 2 * UNROLL, 2 * UNROLL)
        return pltpu.make_async_copy(powers_hbm.at[at], powers.at[at], powers_done.at[s])

    def fetch(s, carry):
        chunk_copy(s).start()
        return carry

    lax.fori_loop(0, steps, fetch, 0)

    got = scores[0]
    for g in range(1, groups):
        got = got + scores[g]
    student = got[0:queries_all, 0:candidates]

    def gather_parts(kind):
        rows = []
        for g in range(groups):
            parts = []
            for part in range(3):
                at = tokens + (kind + part) * query_local
                block = arrived[g, at : at + query_local, 0:candidates]
                parts.append(block.astype(jnp.float32))
            rows.append((parts[0] + parts[1]) + parts[2])
        return jnp.concatenate(rows, axis=0)

    log_teacher = gather_parts(2)
    weight = gather_parts(5)
    shifted = student - jnp.max(student, axis=1, keepdims=True)
    log_student = shifted - jnp.log(jnp.sum(jnp.exp(shifted), axis=1, keepdims=True))
    teacher_prob = jnp.exp(log_teacher)
    spread = jnp.sum(weight * teacher_prob * (log_teacher - log_student), axis=1, keepdims=True)
    numerator = jnp.sum(spread, axis=0, keepdims=True)
    numerator_out[...] = jnp.broadcast_to(numerator, numerator_out.shape)
    weight_sum = got[0:1, candidates : candidates + 1]
    weight_sum_out[...] = jnp.broadcast_to(weight_sum, weight_sum_out.shape)
    scale = query_total / weight_sum
    grad = (weight * scale) * (jnp.exp(log_student) - teacher_prob)

    passage_index = iota((passage_count, candidates), 0)
    lane_query = iota((passage_count, lanes), 1) // query_len
    for tile in range(tiles):
        spread_out = jnp.zeros((passage_count, lanes), jnp.float32)
        for inner in range(per_tile):
            g = tile * groups_per_tile + inner // query_local
            q = inner % query_local
            mine = owned_rows(arrived, tokens, query_local, candidates, g, q, me)
            at = tile * per_tile + inner
            picked = jnp.where(passage_index == mine, grad[at : at + 1], 0.0)
            total = jnp.sum(picked, axis=1, keepdims=True)
            spread_out = jnp.where(lane_query == inner, total, spread_out)
        factors[tile, 0:passage_count, :] = spread_out / summed[tile, 0:passage_count, :]
        factors[tile, passage_count:, :] = jnp.zeros((slots - passage_count, lanes), jnp.float32)
    multiplier[...] = factors[...]

    for one in sums:
        one[...] = jnp.zeros_like(one)

    fetch_rows.wait()

    def step(s, carry):
        chunk_copy(s).wait()
        for u in range(2 * UNROLL):
            b = s * 2 * UNROLL + u
            slot, tile = decode(block_code, b, tiles)
            p = jnp.minimum(slot, passage_count - 1)
            part = powers[b].astype(jnp.float32) * factors[tile, pl.ds(slot, 1), :]
            part = part.astype(jnp.bfloat16)
            sums[u % len(sums)][tile] += lax.dot_general(
                passages[p], part, (((0,), (0,)), ((), ())), preferred_element_type=jnp.float32
            )
        return carry

    lax.fori_loop(0, steps, step, 0)
    for tile in range(tiles):
        back = pair_sums([one[tile] for one in sums]).T.astype(jnp.bfloat16)
        for inner in range(groups_per_tile):
            g = tile * groups_per_tile + inner
            grads_out[g] = back[inner * tokens : (inner + 1) * tokens]


def passage_kernel(
    dims,
    arrived,
    multiplier,
    block_code,
    block_count,
    powers_hbm,
    out_hbm,
    out,
    powers,
    sums,
    queries_all,
    powers_done,
    out_done,
):
    tokens, per_tile_groups = dims
    token_len, passage_count, feature = out.shape
    tiles = queries_all.shape[0]
    padded = powers.shape[1]
    pitch = sums.shape[0] // (passage_count + 1)
    steps = block_count[0, 0]

    def chunk_copy(s):
        at = pl.ds(s * 2 * UNROLL, 2 * UNROLL)
        return pltpu.make_async_copy(powers_hbm.at[at], powers.at[at], powers_done.at[s])

    def fetch(s, carry):
        chunk_copy(s).start()
        return carry

    lax.fori_loop(0, steps, fetch, 0)
    for tile in range(tiles):
        for inner in range(per_tile_groups):
            g = tile * per_tile_groups + inner
            queries_all[tile, inner * tokens : (inner + 1) * tokens, :] = arrived[g, 0:tokens, :]

    def clear(p, carry):
        sums[pl.ds(p * pitch, pitch), :] = jnp.zeros((pitch, feature), jnp.float32)
        return carry

    lax.fori_loop(0, passage_count, clear, 0)

    def step(s, carry):
        chunk_copy(s).wait()
        for u in range(2 * UNROLL):
            b = s * 2 * UNROLL + u
            slot, tile = decode(block_code, b, tiles)
            part = powers[b].astype(jnp.float32) * multiplier[tile, pl.ds(slot, 1), :]
            at = pl.ds(slot * pitch, padded)
            sums[at, :] += jnp.dot(
                part.astype(jnp.bfloat16), queries_all[tile], preferred_element_type=jnp.float32
            )
        return carry

    lax.fori_loop(0, steps, step, 0)

    pieces = out_done.shape[0]
    piece = token_len // pieces
    copies = []
    for k in range(pieces):
        first = k * piece
        last = token_len if k == pieces - 1 else first + piece

        def store(j, carry, first=first):
            for u in range(STORE):
                at = first + j * STORE + u
                out[at] = sums[pl.ds(at, passage_count, stride=pitch), :].astype(out.dtype)
            return carry

        whole = (last - first) // STORE
        lax.fori_loop(0, whole, store, 0)
        for at in range(first + whole * STORE, last):
            out[at] = sums[pl.ds(at, passage_count, stride=pitch), :].astype(out.dtype)
        rows = pl.ds(first, last - first)
        copies.append(pltpu.make_async_copy(out.at[rows], out_hbm.at[rows], out_done.at[k]))
        copies[-1].start()
    for copy in copies:
        copy.wait()


def vmem(count):
    return [pl.BlockSpec(memory_space=VMEM)] * count


def smem(count):
    return [pl.BlockSpec(memory_space=SMEM)] * count


def from_replicas(values, replicas):
    rings = [[(r, r ^ hop) for r in range(replicas)] for hop in range(1, replicas)]
    return [values] + [lax.ppermute(values, "rep", ring) for ring in rings]


def hbm(count):
    return [pl.BlockSpec(memory_space=pltpu.HBM)] * count


def on_device(queries, passages, lengths, cand_ids, owner_map, teacher, weights):
    groups = lax.axis_size("grp")
    replicas = lax.axis_size("rep")
    query_local, _, query_len, feature = queries.shape
    passage_local, _, token_len, _ = passages.shape
    candidates = cand_ids.shape[2]
    tokens = query_local * query_len
    lanes = 128
    per_tile = lanes // query_len
    tiles = groups * tokens // lanes
    padded = round_up(token_len, 16)
    pitch = padded + 9
    ref_count = query_local * candidates
    capacity = groups * (2 * ref_count // groups)
    limit = min(passage_local * tiles, capacity)
    blocks = limit + 3 * UNROLL
    chunks = -(-limit // (2 * UNROLL))
    aux_rows = round_up(KINDS * query_local, 16)
    slots = round_up(passage_local + 1, 8)
    score_rows = round_up(groups * query_local, 8)
    shape = jax.ShapeDtypeStruct
    alone = pltpu.CompilerParams(vmem_limit_bytes=62 * 2**20)
    params = pltpu.CompilerParams(vmem_limit_bytes=52 * 2**20)

    share = pl.pallas_call(
        functools.partial(pack_kernel, passage_local),
        out_shape=shape((groups, tokens + aux_rows, feature), jnp.bfloat16),
        in_specs=vmem(5),
        out_specs=pl.BlockSpec(memory_space=VMEM),
        scratch_shapes=[VMEM((aux_rows, feature), jnp.float32)],
        name="pack",
        compiler_params=alone,
    )(queries.reshape(tokens, feature), cand_ids, owner_map, teacher, weights.T)
    arrived = lax.all_to_all(share, "grp", split_axis=0, concat_axis=0, tiled=True)

    replica_weights = from_replicas(weights.T, replicas)

    rows = pl.pallas_call(
        prepare_kernel,
        out_shape=shape((passage_local, padded, feature), jnp.bfloat16),
        in_specs=hbm(1),
        out_specs=pl.BlockSpec(memory_space=pltpu.HBM),
        scratch_shapes=[
            VMEM((token_len, passage_local, feature), jnp.bfloat16),
            VMEM((passage_local * pitch, feature), jnp.float32),
            VMEM((passage_local, padded, feature), jnp.bfloat16),
            pltpu.SemaphoreType.DMA((PIECES,)),
            pltpu.SemaphoreType.DMA((math.gcd(passage_local, PIECES),)),
        ],
        name="prepare",
        compiler_params=params,
    )(passages[:, 0].transpose(1, 0, 2))

    dims = (tokens, query_local, candidates, per_tile)
    scores, summed, block_code, block_count, powers = (
        pl.pallas_call(
            functools.partial(score_kernel, dims + (replicas,), "grp"),
            out_shape=(
                shape((groups, score_rows, 128), jnp.float32),
                shape((tiles, slots, lanes), jnp.float32),
                shape((1, blocks), jnp.int32),
                shape((1, 1), jnp.int32),
                shape((chunks * 2 * UNROLL, padded, lanes), jnp.bfloat16),
            ),
            in_specs=vmem(1) + smem(1) + vmem(replicas) + hbm(1),
            out_specs=tuple(vmem(2) + smem(2) + hbm(1)),
            scratch_shapes=[
                VMEM((tiles, slots, lanes), jnp.float32),
                VMEM((passage_local, padded, feature), jnp.bfloat16),
                VMEM((tiles, feature, lanes), jnp.bfloat16),
                VMEM((passage_local, 128), jnp.int32),
                SMEM((passage_local, 128), jnp.int32),
                VMEM((2 * padded, lanes), jnp.float32),
                VMEM((UNROLL, padded, lanes), jnp.float32),
                VMEM((UNROLL, padded, lanes), jnp.float32),
                VMEM((UNROLL, lanes), jnp.float32),
                VMEM((UNROLL, lanes), jnp.float32),
                VMEM((chunks * 2 * UNROLL, padded, lanes), jnp.bfloat16),
                pltpu.SemaphoreType.DMA,
                pltpu.SemaphoreType.DMA,
                pltpu.SemaphoreType.DMA((chunks,)),
            ],
            name="score",
            compiler_params=params,
        )(arrived, lengths.T, *replica_weights, rows)
    )
    all_scores = lax.all_to_all(scores, "grp", split_axis=0, concat_axis=0, tiled=True)

    query_total = query_local * groups * replicas
    grads, multiplier, numerator, weight_sum = pl.pallas_call(
        functools.partial(query_kernel, dims + (query_total,), "grp"),
        out_shape=(
            shape((groups, tokens, feature), jnp.bfloat16),
            shape((tiles, slots, lanes), jnp.float32),
            shape((1, 128), jnp.float32),
            shape((1, 128), jnp.float32),
        ),
        in_specs=vmem(3) + smem(2) + hbm(2),
        out_specs=tuple(vmem(4)),
        scratch_shapes=[
            VMEM(rows.shape, jnp.bfloat16),
            VMEM(powers.shape, jnp.bfloat16),
            VMEM((tiles, slots, lanes), jnp.float32),
            pltpu.SemaphoreType.DMA,
            pltpu.SemaphoreType.DMA((chunks,)),
        ]
        + [VMEM((tiles, feature, lanes), jnp.float32)] * SUMS,
        name="query_grad",
        compiler_params=params,
    )(arrived, all_scores, summed, block_code, block_count, rows, powers)
    returned = lax.all_to_all(grads, "grp", split_axis=0, concat_axis=0, tiled=True)

    passage_grad = pl.pallas_call(
        functools.partial(passage_kernel, (tokens, per_tile // query_local)),
        out_shape=shape((token_len, passage_local, feature), jnp.bfloat16),
        in_specs=vmem(2) + smem(2) + hbm(1),
        out_specs=pl.BlockSpec(memory_space=pltpu.HBM),
        scratch_shapes=[
            VMEM((token_len, passage_local, feature), jnp.bfloat16),
            VMEM(powers.shape, jnp.bfloat16),
            VMEM(((passage_local + 1) * pitch, feature), jnp.float32),
            VMEM((tiles, lanes, feature), jnp.bfloat16),
            pltpu.SemaphoreType.DMA((chunks,)),
            pltpu.SemaphoreType.DMA((PIECES,)),
        ],
        name="passage_grad",
        compiler_params=params,
        cost_estimate=pl.CostEstimate(
            flops=2 * limit * padded * lanes * feature,
            bytes_accessed=2 * limit * padded * lanes,
            transcendentals=0,
        ),
    )(arrived, multiplier, block_code, block_count, powers)
    numerators = from_replicas(numerator, replicas)

    loss = pair_sums(numerators)[0, 0] / weight_sum[0, 0]
    query_grad = jnp.sum(returned.astype(jnp.float32), axis=0)
    query_grad = query_grad.reshape(query_local, 1, query_len, feature)
    return (loss, query_grad, passage_grad.transpose(1, 0, 2)[:, None])


def solution(mesh):
    return jax.shard_map(
        on_device,
        mesh=mesh,
        in_specs=(
            P("grp", "rep", None, None),
            P("grp", "rep", None, None),
            P("grp", "rep"),
            P("grp", "rep", None),
            P("rep", None),
            P("grp", "rep", None),
            P("grp", "rep"),
        ),
        out_specs=(P(), P("grp", "rep", None, None), P("grp", "rep", None, None)),
        check_vma=False,
    )
```

profile of v0, /device:TPU:0, one launch (start us, length us, event | category | flops | bytes accessed | tf_op | source)
XLA Modules:
  0.0 59.8 jit_solution(505665019523547355)
XLA Ops:
  0.6 1.6 %pack.1 = bf16[8,80,128]{2,1,0:T(8,128)(2,1)} custom-call(bf16[64,128]{1,0:T(8,128)(2,1)} %bitcast.23, s32[2,1,64]{2,1,0:T(1,128)} %cand_ids.1, s32[1,512]{1,0:T(1,128)} %owner_map.1, f32[2,1,64]{2,1,0:T(1,128)} %teacher.1, f32[1,2]{1,0:T(1,128)} %bitcast.13), custom_call_target="tpu_custom_call" | custom-call | tf_op jit(solution)/shard_map/pack/pallas_call | solution.py:556
  2.2 0.0 copy-start
  2.2 0.0 copy-start.1
  2.2 7.4 %all-to-all-start = ((bf16[8,80,128]{2,1,0:T(8,128)(2,1)}), bf16[8,80,128]{2,1,0:T(8,128)(2,1)S(1)}, u32[]{:S(2)}, u32[]{:S(2)}) async-start(bf16[8,80,128]{2,1,0:T(8,128)(2,1)} %pack.1), calls=%async_computation | async-start | bytes 327680 | tf_op jit(solution)/shard_map/all_to_all | solution.py:565
  9.7 0.7 %collective-permute-start.2 = (f32[1,2]{1,0:T(1,128)}, f32[1,2]{1,0:T(1,128)S(1)}, u32[]{:S(2)}, u32[]{:S(2)}) collective-permute-start(f32[1,2]{1,0:T(1,128)} %bitcast.14), channel_id=1, source_target_pairs={{0,3},{1,2},{2,1},{3,0},{4,7},{5,6},{6,5},{7,4},{8,11},{9,10},{10,... | collective-permute-start | bytes 32 | tf_op jit(solution)/shard_map/ppermute | solution.py:525
  10.3 0.9 %collective-permute-start.1 = (f32[1,2]{1,0:T(1,128)}, f32[1,2]{1,0:T(1,128)S(1)}, u32[]{:S(2)}, u32[]{:S(2)}) collective-permute-start(f32[1,2]{1,0:T(1,128)} %bitcast.15), channel_id=1, source_target_pairs={{0,2},{1,3},{2,0},{3,1},{4,6},{5,7},{6,4},{7,5},{8,10},{9,11},{10,... | collective-permute-start | bytes 32 | tf_op jit(solution)/shard_map/ppermute | solution.py:525
  11.3 0.3 collective-permute-start
  11.5 3.7 %prepare.1.refs_4_.passages_hbm = bf16[64,192,128]{2,1,0:T(8,128)(2,1)} custom-call(bf16[180,64,128]{2,1,0:T(8,128)(2,1)} %bitcast.20), custom_call_target="tpu_custom_call" | custom-call | tf_op jit(solution)/shard_map/prepare/pallas_call | solution.py:569
  15.2 0.0 collective-permute-done.2.refs_3_
  15.2 0.0 collective-permute-done.1.refs_2_
  15.2 0.0 collective-permute-done.refs_1_
  15.3 2.0 %all-to-all-done.arrived = bf16[8,80,128]{2,1,0:T(8,128)(2,1)S(1)} async-done(((bf16[8,80,128]{2,1,0:T(8,128)(2,1)}), bf16[8,80,128]{2,1,0:T(8,128)(2,1)S(1)}, u32[]{:S(2)}, u32[]{:S(2)}) %all-to-all-start) | async-done | bytes 163872 | tf_op jit(solution)/shard_map/all_to_all | solution.py:565
  17.2 0.0 copy-done
  17.3 0.0 copy-done.1
  17.3 8.9 %score.1 = (f32[8,16,128]{2,1,0:T(8,128)S(1)}, f32[4,72,128]{2,1,0:T(8,128)S(1)}, s32[1,298]{1,0:T(1,128)S(1)}, s32[1,1]{1,0:T(1,128)}, bf16[280,192,128]{2,1,0:T(8,128)(2,1)}) custom-call(bf16[8,80,128]{2,1,0:T(8,128)(2,1)S(1)} %all-to-all-done.arrived, s32[1,64]{1,0:T(1,128)S(1)} %bitcast.18, f32[1,2]{1,0:T(1,128)S(1)} %bitcast.17, ...), custom_call_target="tpu_custom_call" | custom-call | tf_op jit(solution)/shard_map/score/pallas_call | solution.py:587
  26.2 11.0 %all_to_all.15.scores = f32[8,16,128]{2,1,0:T(8,128)S(1)} all-to-all(f32[8,16,128]{2,1,0:T(8,128)S(1)} %get-tuple-element.12), channel_id=1, replica_groups=mesh['grp'=8,'rep'=4] {'grp'}, dimensions={0} | all-to-all | bytes 131072 | tf_op jit(solution)/shard_map/all_to_all | solution.py:618
  37.2 7.2 %query_grad.1 = (bf16[8,64,128]{2,1,0:T(8,128)(2,1)}, f32[4,72,128]{2,1,0:T(8,128)S(1)}, f32[1,128]{1,0:T(1,128)S(1)}, f32[1,128]{1,0:T(1,128)S(1)}) custom-call(bf16[8,80,128]{2,1,0:T(8,128)(2,1)S(1)} %all-to-all-done.arrived, f32[8,16,128]{2,1,0:T(8,128)S(1)} %all_to_all.15.scores, f32[4,72,128]{2,1,0:T(8,128)S(1)} %get-tuple-element.13.summed, ...), custom_call_target="tpu_custom_call" | custom-call | tf_op jit(solution)/shard_map/query_grad/pallas_call | solution.py:621
  44.4 0.1 collective-permute-start.5
  44.5 2.3 %collective-permute-start.4 = (f32[1,128]{1,0:T(1,128)S(1)}, f32[1,128]{1,0:T(1,128)S(1)}, u32[]{:S(2)}, u32[]{:S(2)}) collective-permute-start(f32[1,128]{1,0:T(1,128)S(1)} %get-tuple-element.17), channel_id=1, source_target_pairs={{0,2},{1,3},{2,0},{3,1},{4,6},{5,7},{6,4},{7,5},{8,10},{9,11},{10,... | collective-permute-start | bytes 1544 | tf_op jit(solution)/shard_map/ppermute | solution.py:525
  46.8 0.0 collective-permute-start.3
  46.9 3.4 %all-to-all-start.2 = ((bf16[8,64,128]{2,1,0:T(8,128)(2,1)}), bf16[8,64,128]{2,1,0:T(8,128)(2,1)S(1)}, u32[]{:S(2)}, u32[]{:S(2)}) async-start(bf16[8,64,128]{2,1,0:T(8,128)(2,1)} %get-tuple-element.19), calls=%async_computation.2 | async-start | bytes 262144 | tf_op jit(solution)/shard_map/all_to_all | solution.py:642
  50.2 6.7 %passage_grad.1 = bf16[180,64,128]{2,1,0:T(8,128)(2,1)} custom-call(bf16[8,80,128]{2,1,0:T(8,128)(2,1)S(1)} %all-to-all-done.arrived, f32[4,72,128]{2,1,0:T(8,128)S(1)} %get-tuple-element.20.multiplier, s32[1,298]{1,0:T(1,128)S(1)} %get-tuple-element.14.block_code, s32[1,1]{1,0:T(1,128)} %get-tuple-element.15.block_count, ...), custom_call_target="tpu_custom_call" | custom-call | flops 1610612736 | bytes 12582912 | tf_op jit(solution)/shard_map/passage_grad/pallas_call | solution.py:644
  57.0 0.0 collective-permute-done.5
  57.0 0.0 collective-permute-done.4
  57.0 0.0 collective-permute-done.3
  57.1 1.0 %all-to-all-done.2 = bf16[8,64,128]{2,1,0:T(8,128)(2,1)S(1)} async-done(((bf16[8,64,128]{2,1,0:T(8,128)(2,1)}), bf16[8,64,128]{2,1,0:T(8,128)(2,1)S(1)}, u32[]{:S(2)}, u32[]{:S(2)}) %all-to-all-start.2) | async-done | bytes 131104 | tf_op jit(solution)/shard_map/all_to_all | solution.py:642
  58.1 0.6 %convert_reduce_fusion = f32[64,128]{1,0:T(8,128)} fusion(bf16[8,64,128]{2,1,0:T(8,128)(2,1)S(1)} %all-to-all-done.2), kind=kLoop, calls=%fused_computation | loop fusion | flops 122880 | bytes 163840 | tf_op jit(solution)/shard_map/reduce_sum | solution.py:668
  (1 shorter events, 0.0 us)
Async XLA Ops:
  2.2 15.0 %copy-start = (f32[2,1]{0,1:T(1,128)S(1)}, f32[2,1]{0,1:T(1,128)}, u32[]{:S(2)}) copy-start(f32[2,1]{0,1:T(1,128)} %param.13) | copy-start | bytes 28
  2.2 15.0 %copy-start.1 = (s32[64,1]{0,1:T(1,128)S(1)}, s32[64,1]{0,1:T(1,128)}, u32[]{:S(2)}) copy-start(s32[64,1]{0,1:T(1,128)} %param.9) | copy-start | bytes 772
  2.2 15.0 %all-to-all-start = ((bf16[8,80,128]{2,1,0:T(8,128)(2,1)}), bf16[8,80,128]{2,1,0:T(8,128)(2,1)S(1)}, u32[]{:S(2)}, u32[]{:S(2)}) async-start(bf16[8,80,128]{2,1,0:T(8,128)(2,1)} %pack.1), calls=%async_computation | async-start | bytes 327680 | tf_op jit(solution)/shard_map/all_to_all | solution.py:565
  9.7 5.5 %collective-permute-start.2 = (f32[1,2]{1,0:T(1,128)}, f32[1,2]{1,0:T(1,128)S(1)}, u32[]{:S(2)}, u32[]{:S(2)}) collective-permute-start(f32[1,2]{1,0:T(1,128)} %bitcast.14), channel_id=1, source_target_pairs={{0,3},{1,2},{2,1},{3,0},{4,7},{5,6},{6,5},{7,4},{8,11},{9,10},{10,... | collective-permute-start | bytes 32 | tf_op jit(solution)/shard_map/ppermute | solution.py:525
  10.3 4.9 %collective-permute-start.1 = (f32[1,2]{1,0:T(1,128)}, f32[1,2]{1,0:T(1,128)S(1)}, u32[]{:S(2)}, u32[]{:S(2)}) collective-permute-start(f32[1,2]{1,0:T(1,128)} %bitcast.15), channel_id=1, source_target_pairs={{0,2},{1,3},{2,0},{3,1},{4,6},{5,7},{6,4},{7,5},{8,10},{9,11},{10,... | collective-permute-start | bytes 32 | tf_op jit(solution)/shard_map/ppermute | solution.py:525
  11.3 4.0 %collective-permute-start = (f32[1,2]{1,0:T(1,128)}, f32[1,2]{1,0:T(1,128)S(1)}, u32[]{:S(2)}, u32[]{:S(2)}) collective-permute-start(f32[1,2]{1,0:T(1,128)} %bitcast.16), channel_id=1, source_target_pairs={{0,1},{1,0},{2,3},{3,2},{4,5},{5,4},{6,7},{7,6},{8,9},{9,8},{10,11... | collective-permute-start | bytes 32 | tf_op jit(solution)/shard_map/ppermute | solution.py:525
  44.4 12.6 %collective-permute-start.5 = (f32[1,128]{1,0:T(1,128)S(1)}, f32[1,128]{1,0:T(1,128)S(1)}, u32[]{:S(2)}, u32[]{:S(2)}) collective-permute-start(f32[1,128]{1,0:T(1,128)S(1)} %get-tuple-element.17), channel_id=1, source_target_pairs={{0,3},{1,2},{2,1},{3,0},{4,7},{5,6},{6,5},{7,4},{8,11},{9,10},{10,... | collective-permute-start | bytes 1544 | tf_op jit(solution)/shard_map/ppermute | solution.py:525
  44.5 12.5 %collective-permute-start.4 = (f32[1,128]{1,0:T(1,128)S(1)}, f32[1,128]{1,0:T(1,128)S(1)}, u32[]{:S(2)}, u32[]{:S(2)}) collective-permute-start(f32[1,128]{1,0:T(1,128)S(1)} %get-tuple-element.17), channel_id=1, source_target_pairs={{0,2},{1,3},{2,0},{3,1},{4,6},{5,7},{6,4},{7,5},{8,10},{9,11},{10,... | collective-permute-start | bytes 1544 | tf_op jit(solution)/shard_map/ppermute | solution.py:525
  46.8 10.2 %collective-permute-start.3 = (f32[1,128]{1,0:T(1,128)S(1)}, f32[1,128]{1,0:T(1,128)S(1)}, u32[]{:S(2)}, u32[]{:S(2)}) collective-permute-start(f32[1,128]{1,0:T(1,128)S(1)} %get-tuple-element.17), channel_id=1, source_target_pairs={{0,1},{1,0},{2,3},{3,2},{4,5},{5,4},{6,7},{7,6},{8,9},{9,8},{10,11... | collective-permute-start | bytes 1544 | tf_op jit(solution)/shard_map/ppermute | solution.py:525
  46.9 11.2 %all-to-all-start.2 = ((bf16[8,64,128]{2,1,0:T(8,128)(2,1)}), bf16[8,64,128]{2,1,0:T(8,128)(2,1)S(1)}, u32[]{:S(2)}, u32[]{:S(2)}) async-start(bf16[8,64,128]{2,1,0:T(8,128)(2,1)} %get-tuple-element.19), calls=%async_computation.2 | async-start | bytes 262144 | tf_op jit(solution)/shard_map/all_to_all | solution.py:642
where the time goes:
time: 60.3 us; the launch traced here: 59.8 us
  Pallas kernels  28.2 us (47%)
  starting transfers between devices  15.1 us (25%)
  blocking collectives  11 us (18%)
  waiting for transfers between devices  2.96 us (5%)
  between operations  1.95 us (3%)
  other arithmetic  0.64 us (1%)
    all_to_all x1, blocking collectives, on_device(): lax.all_to_all(scores, 'grp', split_axis=0, concat_axis=0, tiled=True)  11 us
    pallas_call x1, Pallas kernels, on_device(): pl.pallas_call(functools.partial(score_kernel, dims + (replicas,), 'grp')...  8.91 us
    all_to_all x1, starting transfers between devices, on_device(): lax.all_to_all(share, 'grp', split_axis=0, concat_axis=0, tiled=True)  7.44 us
    pallas_call x1, Pallas kernels, on_device(): pl.pallas_call(functools.partial(query_kernel, dims + (query_total,), 'gr...  7.22 us
    pallas_call x1, Pallas kernels, on_device(): pl.pallas_call(functools.partial(passage_kernel, (tokens, per_tile // que...  6.75 us
    ppermute x6, starting transfers between devices, from_replicas(): return [values] + [lax.ppermute(values, 'rep', ring) for ring in rings]  4.28 us
    pallas_call x1, Pallas kernels, on_device(): pl.pallas_call(prepare_kernel, out_shape=shape((passage_local, padded, fe...  3.67 us
    all_to_all x1, starting transfers between devices, on_device(): lax.all_to_all(grads, 'grp', split_axis=0, concat_axis=0, tiled=True)  3.37 us
  transfers between devices with their start and end apart: 8, of which 2 were waited for; matrix products, arithmetic and copies ran while one was open for 0% of the time, Pallas kernels for 17%

commit v1 on v0

--- a/solution.py
+++ b/solution.py
@@ -13,7 +13,8 @@
 LOG2E = math.log2(math.e)
 MASKED = -1e30
 KINDS = 8
-UNROLL = 14
+HALF = 7
+UNROLL = 2 * HALF
 SPREAD = 5
 SUMS = 4
 STORE = 5
@@ -245,13 +246,13 @@
     summed[...] = jnp.ones_like(summed)
     penalty[...] = jnp.where(iota(penalty.shape, 0) < padded, 0.0, MASKED)
     to_scalar.wait()
-    steps = list_blocks(flags_scalar, block_code, block_count, passage_count, tiles)
+    steps = (UNROLL // HALF) * list_blocks(flags_scalar, block_code, block_count, passage_count, tiles)
     fetch_rows.wait()
 
     factor = LOG2E / TEMPER
 
     def multiply(first, into, tops):
-        for u in range(UNROLL):
+        for u in range(HALF):
             slot, tile = decode(block_code, first + u, tiles)
             p = jnp.minimum(slot, passage_count - 1)
             products = jnp.dot(passages[p], turned[tile], preferred_element_type=jnp.float32)
@@ -260,7 +261,7 @@
             tops[u : u + 1, :] = jnp.max(products, axis=0, keepdims=True)
 
     def soften(first, held, tops):
-        for u in range(UNROLL):
+        for u in range(HALF):
             slot, tile = decode(block_code, first + u, tiles)
             top = tops[u : u + 1, :]
             raised = jnp.exp2((held[u] - top) * factor)
@@ -269,17 +270,17 @@
             summed[tile, pl.ds(slot, 1), :] = jnp.sum(raised, axis=0, keepdims=True)
 
     def chunk_copy(s):
-        at = pl.ds(s * 2 * UNROLL, 2 * UNROLL)
+        at = pl.ds(s * 2 * HALF, 2 * HALF)
         return pltpu.make_async_copy(powers.at[at], powers_hbm.at[at], powers_done.at[s])
 
     multiply(0, even, even_top)
 
     def step(s, carry):
-        first = s * 2 * UNROLL
-        multiply(first + UNROLL, odd, odd_top)
+        first = s * 2 * HALF
+        multiply(first + HALF, odd, odd_top)
         soften(first, even, even_top)
-        multiply(first + 2 * UNROLL, even, even_top)
-        soften(first + UNROLL, odd, odd_top)
+        multiply(first + 2 * HALF, even, even_top)
+        soften(first + HALF, odd, odd_top)
         chunk_copy(s).start()
         return carry
 
@@ -602,14 +603,14 @@
                 VMEM((passage_local, 128), jnp.int32),
                 SMEM((passage_local, 128), jnp.int32),
                 VMEM((2 * padded, lanes), jnp.float32),
-                VMEM((UNROLL, padded, lanes), jnp.float32),
-                VMEM((UNROLL, padded, lanes), jnp.float32),
-                VMEM((UNROLL, lanes), jnp.float32),
-                VMEM((UNROLL, lanes), jnp.float32),
+                VMEM((HALF, padded, lanes), jnp.float32),
+                VMEM((HALF, padded, lanes), jnp.float32),
+                VMEM((HALF, lanes), jnp.float32),
+                VMEM((HALF, lanes), jnp.float32),
                 VMEM((chunks * 2 * UNROLL, padded, lanes), jnp.bfloat16),
                 pltpu.SemaphoreType.DMA,
                 pltpu.SemaphoreType.DMA,
-                pltpu.SemaphoreType.DMA((chunks,)),
+                pltpu.SemaphoreType.DMA((chunks * UNROLL // HALF,)),
             ],
             name="score",
             compiler_params=params,

time: 60.3 us -> 60.8 us (level)
  no operation moved by 1% of the time
where the time goes in v1:
time: 60.8 us; the launch traced here: 60.4 us
  Pallas kernels  28.3 us (47%)
  starting transfers between devices  15.6 us (26%)
  blocking collectives  10.9 us (18%)
  waiting for transfers between devices  2.96 us (5%)
  between operations  1.95 us (3%)
  other arithmetic  0.64 us (1%)
    all_to_all x1, blocking collectives, on_device(): lax.all_to_all(scores, 'grp', split_axis=0, concat_axis=0, tiled=True)  10.9 us
    pallas_call x1, Pallas kernels, on_device(): pl.pallas_call(functools.partial(score_kernel, dims + (replicas,), 'grp')...  9.1 us
    all_to_all x1, starting transfers between devices, on_device(): lax.all_to_all(share, 'grp', split_axis=0, concat_axis=0, tiled=True)  7.44 us
    pallas_call x1, Pallas kernels, on_device(): pl.pallas_call(functools.partial(query_kernel, dims + (query_total,), 'gr...  7.22 us
    pallas_call x1, Pallas kernels, on_device(): pl.pallas_call(functools.partial(passage_kernel, (tokens, per_tile // que...  6.75 us
    ppermute x6, starting transfers between devices, from_replicas(): return [values] + [lax.ppermute(values, 'rep', ring) for ring in rings]  4.77 us
    pallas_call x1, Pallas kernels, on_device(): pl.pallas_call(prepare_kernel, out_shape=shape((passage_local, padded, fe...  3.67 us
    all_to_all x1, starting transfers between devices, on_device(): lax.all_to_all(grads, 'grp', split_axis=0, concat_axis=0, tiled=True)  3.37 us
  transfers between devices with their start and end apart: 8, of which 2 were waited for; matrix products, arithmetic and copies ran while one was open for 0% of the time, Pallas kernels for 17%

profile of v1, /device:TPU:0, one launch (start us, length us, event | category | flops | bytes accessed | tf_op | source)
XLA Modules:
  0.0 60.4 jit_solution(13556710018137182269)
XLA Ops:
  0.6 1.6 %pack.1 = bf16[8,80,128]{2,1,0:T(8,128)(2,1)} custom-call(bf16[64,128]{1,0:T(8,128)(2,1)} %bitcast.23, s32[2,1,64]{2,1,0:T(1,128)} %cand_ids.1, s32[1,512]{1,0:T(1,128)} %owner_map.1, f32[2,1,64]{2,1,0:T(1,128)} %teacher.1, f32[1,2]{1,0:T(1,128)} %bitcast.13), custom_call_target="tpu_custom_call" | custom-call | tf_op jit(solution)/shard_map/pack/pallas_call | solution.py:557
  2.2 0.0 copy-start
  2.2 0.0 copy-start.1
  2.2 7.4 %all-to-all-start = ((bf16[8,80,128]{2,1,0:T(8,128)(2,1)}), bf16[8,80,128]{2,1,0:T(8,128)(2,1)S(1)}, u32[]{:S(2)}, u32[]{:S(2)}) async-start(bf16[8,80,128]{2,1,0:T(8,128)(2,1)} %pack.1), calls=%async_computation | async-start | bytes 327680 | tf_op jit(solution)/shard_map/all_to_all | solution.py:566
  9.7 0.7 %collective-permute-start.2 = (f32[1,2]{1,0:T(1,128)}, f32[1,2]{1,0:T(1,128)S(1)}, u32[]{:S(2)}, u32[]{:S(2)}) collective-permute-start(f32[1,2]{1,0:T(1,128)} %bitcast.14), channel_id=1, source_target_pairs={{0,3},{1,2},{2,1},{3,0},{4,7},{5,6},{6,5},{7,4},{8,11},{9,10},{10,... | collective-permute-start | bytes 32 | tf_op jit(solution)/shard_map/ppermute | solution.py:526
  10.3 0.9 %collective-permute-start.1 = (f32[1,2]{1,0:T(1,128)}, f32[1,2]{1,0:T(1,128)S(1)}, u32[]{:S(2)}, u32[]{:S(2)}) collective-permute-start(f32[1,2]{1,0:T(1,128)} %bitcast.15), channel_id=1, source_target_pairs={{0,2},{1,3},{2,0},{3,1},{4,6},{5,7},{6,4},{7,5},{8,10},{9,11},{10,... | collective-permute-start | bytes 32 | tf_op jit(solution)/shard_map/ppermute | solution.py:526
  11.3 0.3 collective-permute-start
  11.5 3.7 %prepare.1.refs_4_.passages_hbm = bf16[64,192,128]{2,1,0:T(8,128)(2,1)} custom-call(bf16[180,64,128]{2,1,0:T(8,128)(2,1)} %bitcast.20), custom_call_target="tpu_custom_call" | custom-call | tf_op jit(solution)/shard_map/prepare/pallas_call | solution.py:570
  15.2 0.0 collective-permute-done.2.refs_3_
  15.2 0.0 collective-permute-done.1.refs_2_
  15.2 0.0 collective-permute-done.refs_1_
  15.3 2.0 %all-to-all-done.arrived = bf16[8,80,128]{2,1,0:T(8,128)(2,1)S(1)} async-done(((bf16[8,80,128]{2,1,0:T(8,128)(2,1)}), bf16[8,80,128]{2,1,0:T(8,128)(2,1)S(1)}, u32[]{:S(2)}, u32[]{:S(2)}) %all-to-all-start) | async-done | bytes 163872 | tf_op jit(solution)/shard_map/all_to_all | solution.py:566
  17.2 0.0 copy-done
  17.3 0.0 copy-done.1
  17.3 9.1 %score.1 = (f32[8,16,128]{2,1,0:T(8,128)S(1)}, f32[4,72,128]{2,1,0:T(8,128)S(1)}, s32[1,298]{1,0:T(1,128)S(1)}, s32[1,1]{1,0:T(1,128)}, bf16[280,192,128]{2,1,0:T(8,128)(2,1)}) custom-call(bf16[8,80,128]{2,1,0:T(8,128)(2,1)S(1)} %all-to-all-done.arrived, s32[1,64]{1,0:T(1,128)S(1)} %bitcast.18, f32[1,2]{1,0:T(1,128)S(1)} %bitcast.17, ...), custom_call_target="tpu_custom_call" | custom-call | tf_op jit(solution)/shard_map/score/pallas_call | solution.py:588
  26.4 10.9 %all_to_all.15.scores = f32[8,16,128]{2,1,0:T(8,128)S(1)} all-to-all(f32[8,16,128]{2,1,0:T(8,128)S(1)} %get-tuple-element.12), channel_id=1, replica_groups=mesh['grp'=8,'rep'=4] {'grp'}, dimensions={0} | all-to-all | bytes 131072 | tf_op jit(solution)/shard_map/all_to_all | solution.py:619
  37.2 7.2 %query_grad.1 = (bf16[8,64,128]{2,1,0:T(8,128)(2,1)}, f32[4,72,128]{2,1,0:T(8,128)S(1)}, f32[1,128]{1,0:T(1,128)S(1)}, f32[1,128]{1,0:T(1,128)S(1)}) custom-call(bf16[8,80,128]{2,1,0:T(8,128)(2,1)S(1)} %all-to-all-done.arrived, f32[8,16,128]{2,1,0:T(8,128)S(1)} %all_to_all.15.scores, f32[4,72,128]{2,1,0:T(8,128)S(1)} %get-tuple-element.13.summed, ...), custom_call_target="tpu_custom_call" | custom-call | tf_op jit(solution)/shard_map/query_grad/pallas_call | solution.py:622
  44.5 0.1 collective-permute-start.5
  44.5 2.8 %collective-permute-start.4 = (f32[1,128]{1,0:T(1,128)S(1)}, f32[1,128]{1,0:T(1,128)S(1)}, u32[]{:S(2)}, u32[]{:S(2)}) collective-permute-start(f32[1,128]{1,0:T(1,128)S(1)} %get-tuple-element.17), channel_id=1, source_target_pairs={{0,2},{1,3},{2,0},{3,1},{4,6},{5,7},{6,4},{7,5},{8,10},{9,11},{10,... | collective-permute-start | bytes 1544 | tf_op jit(solution)/shard_map/ppermute | solution.py:526
  47.3 0.0 collective-permute-start.3
  47.4 3.4 %all-to-all-start.2 = ((bf16[8,64,128]{2,1,0:T(8,128)(2,1)}), bf16[8,64,128]{2,1,0:T(8,128)(2,1)S(1)}, u32[]{:S(2)}, u32[]{:S(2)}) async-start(bf16[8,64,128]{2,1,0:T(8,128)(2,1)} %get-tuple-element.19), calls=%async_computation.2 | async-start | bytes 262144 | tf_op jit(solution)/shard_map/all_to_all | solution.py:643
  50.8 6.7 %passage_grad.1 = bf16[180,64,128]{2,1,0:T(8,128)(2,1)} custom-call(bf16[8,80,128]{2,1,0:T(8,128)(2,1)S(1)} %all-to-all-done.arrived, f32[4,72,128]{2,1,0:T(8,128)S(1)} %get-tuple-element.20.multiplier, s32[1,298]{1,0:T(1,128)S(1)} %get-tuple-element.14.block_code, s32[1,1]{1,0:T(1,128)} %get-tuple-element.15.block_count, ...), custom_call_target="tpu_custom_call" | custom-call | flops 1610612736 | bytes 12582912 | tf_op jit(solution)/shard_map/passage_grad/pallas_call | solution.py:645
  57.5 0.0 collective-permute-done.5
  57.5 0.0 collective-permute-done.4
  57.5 0.0 collective-permute-done.3
  57.6 1.0 %all-to-all-done.2 = bf16[8,64,128]{2,1,0:T(8,128)(2,1)S(1)} async-done(((bf16[8,64,128]{2,1,0:T(8,128)(2,1)}), bf16[8,64,128]{2,1,0:T(8,128)(2,1)S(1)}, u32[]{:S(2)}, u32[]{:S(2)}) %all-to-all-start.2) | async-done | bytes 131104 | tf_op jit(solution)/shard_map/all_to_all | solution.py:643
  58.6 0.6 %convert_reduce_fusion = f32[64,128]{1,0:T(8,128)} fusion(bf16[8,64,128]{2,1,0:T(8,128)(2,1)S(1)} %all-to-all-done.2), kind=kLoop, calls=%fused_computation | loop fusion | flops 122880 | bytes 163840 | tf_op jit(solution)/shard_map/reduce_sum | solution.py:669
  (1 shorter events, 0.0 us)
Async XLA Ops:
  2.2 15.0 %copy-start = (f32[2,1]{0,1:T(1,128)S(1)}, f32[2,1]{0,1:T(1,128)}, u32[]{:S(2)}) copy-start(f32[2,1]{0,1:T(1,128)} %param.13) | copy-start | bytes 28
  2.2 15.0 %copy-start.1 = (s32[64,1]{0,1:T(1,128)S(1)}, s32[64,1]{0,1:T(1,128)}, u32[]{:S(2)}) copy-start(s32[64,1]{0,1:T(1,128)} %param.9) | copy-start | bytes 772
  2.2 15.0 %all-to-all-start = ((bf16[8,80,128]{2,1,0:T(8,128)(2,1)}), bf16[8,80,128]{2,1,0:T(8,128)(2,1)S(1)}, u32[]{:S(2)}, u32[]{:S(2)}) async-start(bf16[8,80,128]{2,1,0:T(8,128)(2,1)} %pack.1), calls=%async_computation | async-start | bytes 327680 | tf_op jit(solution)/shard_map/all_to_all | solution.py:566
  9.7 5.5 %collective-permute-start.2 = (f32[1,2]{1,0:T(1,128)}, f32[1,2]{1,0:T(1,128)S(1)}, u32[]{:S(2)}, u32[]{:S(2)}) collective-permute-start(f32[1,2]{1,0:T(1,128)} %bitcast.14), channel_id=1, source_target_pairs={{0,3},{1,2},{2,1},{3,0},{4,7},{5,6},{6,5},{7,4},{8,11},{9,10},{10,... | collective-permute-start | bytes 32 | tf_op jit(solution)/shard_map/ppermute | solution.py:526
  10.3 4.9 %collective-permute-start.1 = (f32[1,2]{1,0:T(1,128)}, f32[1,2]{1,0:T(1,128)S(1)}, u32[]{:S(2)}, u32[]{:S(2)}) collective-permute-start(f32[1,2]{1,0:T(1,128)} %bitcast.15), channel_id=1, source_target_pairs={{0,2},{1,3},{2,0},{3,1},{4,6},{5,7},{6,4},{7,5},{8,10},{9,11},{10,... | collective-permute-start | bytes 32 | tf_op jit(solution)/shard_map/ppermute | solution.py:526
  11.3 4.0 %collective-permute-start = (f32[1,2]{1,0:T(1,128)}, f32[1,2]{1,0:T(1,128)S(1)}, u32[]{:S(2)}, u32[]{:S(2)}) collective-permute-start(f32[1,2]{1,0:T(1,128)} %bitcast.16), channel_id=1, source_target_pairs={{0,1},{1,0},{2,3},{3,2},{4,5},{5,4},{6,7},{7,6},{8,9},{9,8},{10,11... | collective-permute-start | bytes 32 | tf_op jit(solution)/shard_map/ppermute | solution.py:526
  44.5 13.1 %collective-permute-start.5 = (f32[1,128]{1,0:T(1,128)S(1)}, f32[1,128]{1,0:T(1,128)S(1)}, u32[]{:S(2)}, u32[]{:S(2)}) collective-permute-start(f32[1,128]{1,0:T(1,128)S(1)} %get-tuple-element.17), channel_id=1, source_target_pairs={{0,3},{1,2},{2,1},{3,0},{4,7},{5,6},{6,5},{7,4},{8,11},{9,10},{10,... | collective-permute-start | bytes 1544 | tf_op jit(solution)/shard_map/ppermute | solution.py:526
  44.5 13.0 %collective-permute-start.4 = (f32[1,128]{1,0:T(1,128)S(1)}, f32[1,128]{1,0:T(1,128)S(1)}, u32[]{:S(2)}, u32[]{:S(2)}) collective-permute-start(f32[1,128]{1,0:T(1,128)S(1)} %get-tuple-element.17), channel_id=1, source_target_pairs={{0,2},{1,3},{2,0},{3,1},{4,6},{5,7},{6,4},{7,5},{8,10},{9,11},{10,... | collective-permute-start | bytes 1544 | tf_op jit(solution)/shard_map/ppermute | solution.py:526
  47.3 10.2 %collective-permute-start.3 = (f32[1,128]{1,0:T(1,128)S(1)}, f32[1,128]{1,0:T(1,128)S(1)}, u32[]{:S(2)}, u32[]{:S(2)}) collective-permute-start(f32[1,128]{1,0:T(1,128)S(1)} %get-tuple-element.17), channel_id=1, source_target_pairs={{0,1},{1,0},{2,3},{3,2},{4,5},{5,4},{6,7},{7,6},{8,9},{9,8},{10,11... | collective-permute-start | bytes 1544 | tf_op jit(solution)/shard_map/ppermute | solution.py:526
  47.4 11.2 %all-to-all-start.2 = ((bf16[8,64,128]{2,1,0:T(8,128)(2,1)}), bf16[8,64,128]{2,1,0:T(8,128)(2,1)S(1)}, u32[]{:S(2)}, u32[]{:S(2)}) async-start(bf16[8,64,128]{2,1,0:T(8,128)(2,1)} %get-tuple-element.19), calls=%async_computation.2 | async-start | bytes 262144 | tf_op jit(solution)/shard_map/all_to_all | solution.py:643
